TPU v7x, 32 devices: a whole 2x2x4 slice. The times are simulated.
32 devices in a mesh: dp: 8 (over y, x, core), tensor: 4 (over z).
Axes of the slice: x: 2, y: 2, z: 4, core: 2. Of those that a mesh axis runs over, the one named last changes fastest.
Arguments:
- tokens: bfloat16 [4096, 2304], P(('dp', 'tensor')), may hold values from -6 to 6
- cotangent: bfloat16 [4096, 4096], P('dp', 'tensor'), may hold values from -6 to 6
- pre_gain: float32 [2304], replicated, may hold values from 0.25 to 1.75
- w_query: bfloat16 [2304, 4096], P('dp', 'tensor'), may hold values from -0.375 to 0.375
- key_weight: bfloat16 [2304, 2048], P('dp', 'tensor'), may hold values from -0.375 to 0.375
- value_weight: bfloat16 [2304, 2048], P('dp', 'tensor'), may hold values from -0.125 to 0.125
Outputs:
- attended: bfloat16 [4096, 4096], P('dp', 'tensor')
- grad_tokens: bfloat16 [4096, 2304], P(('dp', 'tensor'))
- grad_query: float32 [2304, 4096], P('dp', 'tensor')
- grad_key: float32 [2304, 2048], P('dp', 'tensor')
- grad_value: float32 [2304, 2048], P('dp', 'tensor')
- grad_pre_gain: float32 [2304], replicated
All inputs are finite; a program needn't handle non-finite values.
Results may differ from a plain program's by a relative error of at most 0.019.
The roundings to bfloat16 on the way count: a program that leaves them out, or rounds other values in their place, can miss the bound.
Values may be sent and summed in bfloat16 or wider, within the bound.
A program may use at most 192 MiB of HBM per device.

v0:
```python
import jax
import jax.numpy as jnp
from jax import lax
from jax.sharding import PartitionSpec as P

HEAD_SIZE = 128
SEQ_LEN = 64
EPS = 1e-06
CAP = 50.0
BASE = 10000.0
query_scalar = 144.0


def rotary_tables(segment_length, half):
    places = jnp.arange(segment_length, dtype=jnp.float32)[:, None]
    freqs = BASE ** (-jnp.arange(half, dtype=jnp.float32) / half)
    angles = places * freqs[None, :]
    return (jnp.cos(angles)[:, None, :], jnp.sin(angles)[:, None, :])


def rotate(values, cosine_table, sine_table):
    half = values.shape[-1] // 2
    first, second = (values[..., :half], values[..., half:])
    return jnp.concatenate(
        [first * cosine_table - second * sine_table, second * cosine_table + first * sine_table], -1
    )


def inverse_rotation(values, cosine_table, sine_table):
    half = values.shape[-1] // 2
    first, second = (values[..., :half], values[..., half:])
    return jnp.concatenate(
        [first * cosine_table + second * sine_table, second * cosine_table - first * sine_table], -1
    )


def attend_forward(query, key, value):
    repeat = query.shape[1] // key.shape[1]
    keys = jnp.repeat(key, repeat, axis=1)
    values = jnp.repeat(value, repeat, axis=1)
    factor = query_scalar ** (-0.5)
    raw = jnp.einsum("qhd,khd->hqk", query, keys, preferred_element_type=jnp.float32) * factor
    bent = jnp.tanh(raw / CAP)
    capped = CAP * bent
    segment_length = query.shape[0]
    causal = jnp.arange(segment_length)[None, :] <= jnp.arange(segment_length)[:, None]
    raised = jnp.where(causal[None], jnp.exp(capped), 0.0)
    weights = raised / jnp.sum(raised, -1, keepdims=True)
    probs = weights.astype(jnp.bfloat16)
    attended = jnp.einsum("hqk,khd->qhd", probs, values, preferred_element_type=jnp.float32).astype(
        jnp.bfloat16
    )
    return (attended, weights, probs, bent)


def attend_backward(d_attended, query, key, value, weights, probs, bent):
    repeat = query.shape[1] // key.shape[1]
    keys = jnp.repeat(key, repeat, axis=1)
    values = jnp.repeat(value, repeat, axis=1)
    factor = query_scalar ** (-0.5)
    d_probs = jnp.einsum("qhd,khd->hqk", d_attended, values, preferred_element_type=jnp.float32)
    d_capped = weights * (d_probs - jnp.sum(weights * d_probs, -1, keepdims=True))
    d_scores = (d_capped * (1.0 - bent * bent) * factor).astype(jnp.bfloat16)
    query_back = jnp.einsum("hqk,khd->qhd", d_scores, keys, preferred_element_type=jnp.float32)
    key_heads = jnp.einsum("hqk,qhd->khd", d_scores, query, preferred_element_type=jnp.float32)
    value_heads = jnp.einsum("hqk,qhd->khd", probs, d_attended, preferred_element_type=jnp.float32)
    segment_length, heads, width = query.shape
    key_rotated_back = key_heads.reshape(segment_length, heads // repeat, repeat, width).sum(2)
    value_returned = value_heads.reshape(segment_length, heads // repeat, repeat, width).sum(2)
    return (query_back, key_rotated_back, value_returned)


def segment_pass(query, key, value, d_attended):
    attended, weights, probs, bent = attend_forward(query, key, value)
    query_back, key_rotated_back, value_returned = attend_backward(
        d_attended, query, key, value, weights, probs, bent
    )
    return (attended, query_back, key_rotated_back, value_returned)


def per_device(tokens, cotangent, pre_gain, w_query, key_weight, value_weight):
    contract_first = (((0,), (0,)), ((), ()))
    contract_last = (((1,), (1,)), ((), ()))
    rows_f = tokens.astype(jnp.float32)
    inv_one = lax.rsqrt(jnp.mean(rows_f * rows_f, -1, keepdims=True) + EPS)
    unit_one = rows_f * inv_one
    normed_input = (unit_one * pre_gain).astype(jnp.bfloat16)
    gathered = lax.all_gather(normed_input, "tensor", axis=0, tiled=True)
    segment_length = gathered.shape[0]
    token_span = SEQ_LEN
    pieces_count = segment_length // token_span
    heads_query = w_query.shape[1] // HEAD_SIZE
    heads_key = key_weight.shape[1] // HEAD_SIZE
    pieces = (
        lax.all_gather(w_query, "dp", axis=0, tiled=True),
        lax.all_gather(key_weight, "dp", axis=0, tiled=True),
        lax.all_gather(value_weight, "dp", axis=0, tiled=True),
    )
    query_raw, key_unrotated, value_projected = tuple(
        (jnp.dot(gathered, piece, preferred_element_type=jnp.float32) for piece in pieces)
    )
    cosine_table, sine_table = rotary_tables(token_span, HEAD_SIZE // 2)
    query = rotate(
        query_raw.reshape(pieces_count, token_span, heads_query, HEAD_SIZE),
        cosine_table,
        sine_table,
    ).astype(jnp.bfloat16)
    key = rotate(
        key_unrotated.reshape(pieces_count, token_span, heads_key, HEAD_SIZE),
        cosine_table,
        sine_table,
    ).astype(jnp.bfloat16)
    value = value_projected.reshape(pieces_count, token_span, heads_key, HEAD_SIZE).astype(
        jnp.bfloat16
    )
    d_attended = cotangent.reshape(pieces_count, token_span, heads_query, HEAD_SIZE)
    attended, query_back, key_rotated_back, value_returned = jax.vmap(segment_pass)(
        query, key, value, d_attended
    )
    attended_flat = attended.reshape(segment_length, heads_query * HEAD_SIZE)
    d_query = (
        inverse_rotation(query_back, cosine_table, sine_table)
        .astype(jnp.bfloat16)
        .reshape(segment_length, heads_query * HEAD_SIZE)
    )
    key_gradient = (
        inverse_rotation(key_rotated_back, cosine_table, sine_table)
        .astype(jnp.bfloat16)
        .reshape(segment_length, heads_key * HEAD_SIZE)
    )
    value_gradient = value_returned.astype(jnp.bfloat16).reshape(
        segment_length, heads_key * HEAD_SIZE
    )
    back_query, back_key, back_value = (
        lax.all_gather(w_query, "dp", axis=0, tiled=True),
        lax.all_gather(key_weight, "dp", axis=0, tiled=True),
        lax.all_gather(value_weight, "dp", axis=0, tiled=True),
    )
    joined = jnp.concatenate([d_query, key_gradient, value_gradient], 1)
    block = gathered
    grads = lax.psum_scatter(
        lax.dot_general(block, joined, contract_first, preferred_element_type=jnp.float32).astype(
            jnp.bfloat16
        ),
        "dp",
        scatter_dimension=0,
        tiled=True,
    ).astype(jnp.float32)
    width_query = w_query.shape[1]
    width_key = key_weight.shape[1]
    grad_query = grads[:, :width_query]
    grad_key = grads[:, width_query : width_query + width_key]
    grad_value = grads[:, width_query + width_key :]
    total = jnp.zeros((tokens.shape[0] * lax.axis_size("tensor"), gathered.shape[1]), jnp.float32)
    for grad_part, weight in (
        (d_query, back_query),
        (key_gradient, back_key),
        (value_gradient, back_value),
    ):
        block = grad_part
        total = total + lax.dot_general(
            block, weight, contract_last, preferred_element_type=jnp.float32
        )
    d_normed = lax.psum_scatter(
        total.astype(jnp.bfloat16), "tensor", scatter_dimension=0, tiled=True
    ).astype(jnp.float32)
    pre_part = jnp.sum(d_normed * unit_one, 0)
    scaled_in = d_normed * pre_gain
    grad_tokens = (
        inv_one * (scaled_in - unit_one * jnp.mean(scaled_in * unit_one, -1, keepdims=True))
    ).astype(jnp.bfloat16)
    grad_pre = lax.psum(pre_part, ("dp", "tensor"))
    return (attended_flat, grad_tokens, grad_query, grad_key, grad_value, grad_pre)


def solution(mesh):
    placed = (
        P(("dp", "tensor"), None),
        P("dp", "tensor"),
        P(),
        P("dp", "tensor"),
        P("dp", "tensor"),
        P("dp", "tensor"),
    )
    return jax.shard_map(
        per_device,
        mesh=mesh,
        in_specs=placed,
        out_specs=(
            P("dp", "tensor"),
            P(("dp", "tensor"), None),
            P("dp", "tensor"),
            P("dp", "tensor"),
            P("dp", "tensor"),
            P(),
        ),
        check_vma=False,
    )
```

profile of v0, /device:TPU:0, one launch (start us, length us, event | category | flops | bytes accessed | tf_op | source)
XLA Modules:
  0.0 347.0 jit_solution(11530087274163512373)
XLA Ops:
  7.2 1.3 fusion.22
  8.6 2.1 fusion.20
  10.7 0.0 all-gather.7.cloned.1.call-start
  10.7 0.7 all-gather.7.cloned.1.call-update
  11.5 0.7 all-gather.11.cloned.1.call-update
  12.2 0.5 all-gather.9.cloned.1.call-update
  12.8 0.0 reduce-scatter.3.cloned.1.call-start
  12.8 0.3 copy.62
  13.1 0.1 fusion.34
  13.3 50.3 %all-gather.5.cloned.1.call-done = bf16[512,2304]{1,0:T(8,128)(2,1)} async-done(((bf16[128,2304]{1,0:T(8,128)(2,1)}), bf16[512,2304]{1,0:T(8,128)(2,1)}) %all-gather.5.cloned.1.call-update) | async-done | bytes 2359312 | tf_op jit(solution)/shard_map/all_gather | solution.py:88
  63.6 29.6 %all-gather.7.cloned.1.call-done = bf16[2304,512]{1,0:T(8,128)(2,1)} async-done(((bf16[288,512]{1,0:T(8,128)(2,1)}), bf16[2304,512]{1,0:T(8,128)(2,1)}) %all-gather.7.cloned.1.call-update) | async-done | bytes 2359312 | tf_op jit(solution)/shard_map/all_gather | solution.py:97
  93.1 3.8 %convolution_convert_fusion.2 = bf16[512,512]{1,0:T(8,128)(2,1)S(1)} fusion(bf16[512,2304]{1,0:T(8,128)(2,1)} %all-gather.5.cloned.1.call-done, bf16[2304,512]{1,0:T(8,128)(2,1)} %all-gather.7.cloned.1.call-done), kind=kOutput, calls=%fused_computation.36 | convolution fusion | flops 1208221696 | bytes 5242880 | tf_op jit(solution)/shard_map/dot_general | solution.py:100
  96.9 0.1 convert_element_type.61
  97.0 0.1 copy.41
  97.1 26.8 %all-gather.11.cloned.1.call-done = bf16[2304,512]{1,0:T(8,128)(2,1)} async-done(((bf16[288,512]{1,0:T(8,128)(2,1)}), bf16[2304,512]{1,0:T(8,128)(2,1)}) %all-gather.11.cloned.1.call-update) | async-done | bytes 2359312 | tf_op jit(solution)/shard_map/all_gather | solution.py:96
  123.9 4.7 %fusion.56 = f32[512,512]{1,0:T(8,128)} fusion(bf16[512,2304]{1,0:T(8,128)(2,1)} %all-gather.5.cloned.1.call-done, bf16[2304,512]{1,0:T(8,128)(2,1)} %all-gather.11.cloned.1.call-done), kind=kOutput, calls=%fused_computation.86 | convolution fusion | flops 1207959552 | bytes 5767168 | tf_op jit(solution)/shard_map/dot_general | solution.py:100
  128.6 1.6 reshape.112
  130.2 0.6 fusion.55
  130.8 0.3 subtract_convert_fusion.3
  131.2 0.3 pad_maximum_fusion.2
  131.5 0.2 broadcast_in_dim.12
  131.7 1.0 copy-done.4
  132.7 2.0 fusion.28
  134.7 29.7 %all-gather.9.cloned.1.call-done = bf16[2304,1024]{1,0:T(8,128)(2,1)} async-done(((bf16[288,1024]{1,0:T(8,128)(2,1)}), bf16[2304,1024]{1,0:T(8,128)(2,1)}) %all-gather.9.cloned.1.call-update) | async-done | bytes 4718608 | tf_op jit(solution)/shard_map/all_gather | solution.py:95
  164.5 5.3 %convolution_bitcast_fusion = f32[64,8,8,128]{3,1,2,0:T(8,128)S(1)} fusion(bf16[512,2304]{1,0:T(8,128)(2,1)} %all-gather.5.cloned.1.call-done, bf16[2304,1024]{1,0:T(8,128)(2,1)} %all-gather.9.cloned.1.call-done), kind=kOutput, calls=%fused_computation.22 | convolution fusion | flops 2415919104 | bytes 9175040 | tf_op jit(solution)/shard_map/dot_general | solution.py:100
  169.8 0.5 copy.60
  170.3 0.7 fusion.53
  171.0 0.9 subtract_convert_fusion.1
  171.9 0.2 broadcast_in_dim.18
  172.1 2.7 fusion.12
  174.9 7.5 %fusion.25 = f32[8,8,128,64]{2,3,1,0:T(8,128)} fusion(f32[8,8,64,64]{3,2,1,0:T(8,128)} %fusion.28, f32[8,8,64,64]{2,3,1,0:T(8,128)} %get-tuple-element.25, bf16[8,64,8,64]{3,1,2,0:T(8,128)(2,1)} %copy-done.8, bf16[8,64,8,64]{3,1,2,0:T(8,128)(2,1)S(1)} %get-tuple-element.8, f32[8,8,64]{2,1,0:T(8,128)S(1)} %get-tuple-element.24, ...), kind=kOutput, calls=%fused_computation.52 | convolution fusion | flops 73404480 | bytes 5263360 | tf_op jit(solution)/shard_map/vmap(hqk,qhd->khd)/dot_general | solution.py:65
  182.4 5.8 %convolution_bitcast_fusion.1 = f32[8,64,8,128]{3,1,2,0:T(8,128)S(1)} fusion(bf16[8,64,8,128]{3,1,2,0:T(8,128)(2,1)} %bitcast.91, f32[8,8,64,64]{3,2,1,0:T(8,128)} %fusion.28, f32[8,8,64,64]{2,3,1,0:T(8,128)} %get-tuple-element.25, f32[8,8,64]{2,1,0:T(8,128)S(1)} %get-tuple-element.24, pred[64,64]{0,1:T(8,128)(4,1)S(1)} %iota_compare_fusion), kind=kOutput, calls=%fused_computation.23 | convolution fusion | flops 71307328 | bytes 5263360 | tf_op jit(solution)/shard_map/vmap(hqk,khd->qhd)/dot_general | solution.py:64
  188.2 3.7 %fusion.26 = f32[8,8,64,128]{3,2,1,0:T(8,128)} fusion(bf16[8,64,8,128]{3,2,1,0:T(8,128)(2,1)S(1)} %bitcast.87, f32[8,8,64,64]{2,3,1,0:T(8,128)} %get-tuple-element.25, f32[8,8,64]{2,1,0:T(8,128)S(1)} %get-tuple-element.24, pred[64,64]{0,1:T(8,128)(4,1)S(1)} %iota_compare_fusion), kind=kOutput, calls=%fused_computation.53 | convolution fusion | flops 68419584 | bytes 4214784 | tf_op jit(solution)/shard_map/vmap(hqk,qhd->khd)/dot_general | solution.py:66
  191.9 1.9 reduce_sum.66
  193.8 2.7 reduce_sum.67
  196.5 1.5 copy.53
  197.9 0.4 add_convert_fusion.2
  198.4 0.8 add_convert_fusion
  199.2 0.6 pad_maximum_fusion.1
  199.8 0.9 copy.50
  200.7 0.3 pad_maximum_fusion.3
  201.0 0.4 copy.51
  201.5 2.7 fusion.46
  204.2 1.4 convolution_add_fusion.1
  205.6 0.2 copy-done.6
  205.8 2.9 fusion.1
  208.7 0.0 reduce-scatter.5.cloned.1.call-start
  208.8 0.3 copy.85
  209.0 0.7 copy-done.3
  209.7 0.1 copy_bitcast_fusion.2
  209.9 0.7 copy-done.12
  210.5 7.8 %convolution_convert_fusion = bf16[2304,2048]{1,0:T(8,128)(2,1)} fusion(bf16[512,2304]{1,0:T(8,128)(2,1)S(1)} %copy-done.12, bf16[512,512]{1,0:T(8,128)(2,1)S(1)} %get-tuple-element.26, bf16[512,512]{1,0:T(8,128)(2,1)S(1)} %get-tuple-element.27, bf16[512,1024]{1,0:T(8,128)(2,1)S(1)} %bitcast.94), kind=kOutput, calls=%fused_computation.1 | convolution fusion | flops 4842848256 | bytes 13893632 | tf_op jit(solution)/shard_map/dot_general | solution.py:142
  218.4 1.2 copy-done.5
  219.6 0.7 copy-done.13
  220.3 0.9 fusion.17
  221.1 0.7 copy.47
  221.8 1.2 copy.86
  223.1 33.5 %reduce-scatter.3.cloned.1.call-done = bf16[128,2304]{1,0:T(8,128)(2,1)} async-done(((bf16[512,2304]{1,0:T(8,128)(2,1)}), bf16[128,2304]{1,0:T(8,128)(2,1)}) %reduce-scatter.3.cloned.1.call-update) | async-done | bytes 589840 | tf_op jit(solution)/shard_map/reduce_scatter | solution.py:164
  256.6 1.5 fusion.23
  258.1 40.3 %psum.7 = f32[2304]{0:T(1024)} all-reduce(f32[2304]{0:T(1024)S(1)} %get-tuple-element.6), channel_id=1, replica_groups=mesh['dp'=8,'tensor'=4] {'dp','tensor'}, use_global_device_ids=true, to_apply=%region_9.10 | all-reduce | flops 2304 | bytes 18432 | tf_op jit(solution)/shard_map/psum | solution.py:172
  298.4 2.3 fusion.19
  300.7 36.1 %reduce-scatter.5.cloned.1.call-done = bf16[288,2048]{1,0:T(8,128)(2,1)} async-done(((bf16[2304,2048]{1,0:T(8,128)(2,1)}), bf16[288,2048]{1,0:T(8,128)(2,1)}) %reduce-scatter.5.cloned.1.call-update) | async-done | bytes 1179664 | tf_op jit(solution)/shard_map/reduce_scatter | solution.py:141
  336.7 2.3 slice.52
  339.0 1.2 fusion.54
  (37 shorter events, 0.3 us)
Async XLA Ops:
  7.2 5.6 %copy-start.10 = (bf16[512,1024]{1,0:T(8,128)(2,1)S(1)}, bf16[512,1024]{1,0:T(8,128)(2,1)}, u32[]{:S(2)}) copy-start(bf16[512,1024]{1,0:T(8,128)(2,1)} %param.7) | copy-start | bytes 3145732
  7.2 56.4 %all-gather.5.cloned.1.call-start = ((), (), s32[]{:S(2)}) async-start(), calls=%async_computation.2 | async-start | bytes 2949120 | tf_op jit(solution)/shard_map/all_gather | solution.py:88
  10.7 82.4 %all-gather.7.cloned.1.call-start = ((), (), s32[]{:S(2)}) async-start(), calls=%async_computation.3 | async-start | bytes 2654208 | tf_op jit(solution)/shard_map/all_gather | solution.py:97
  11.4 112.5 %all-gather.11.cloned.1.call-start = ((), (), s32[]{:S(2)}) async-start(), calls=%async_computation.5 | async-start | bytes 2654208 | tf_op jit(solution)/shard_map/all_gather | solution.py:96
  12.2 152.3 %all-gather.9.cloned.1.call-start = ((), (), s32[]{:S(2)}) async-start(), calls=%async_computation.4 | async-start | bytes 5308416 | tf_op jit(solution)/shard_map/all_gather | solution.py:95
  12.8 243.8 %reduce-scatter.3.cloned.1.call-start = ((), (), s32[]{:S(2)}) async-start(), calls=%async_computation.6 | async-start | bytes 2949120 | tf_op jit(solution)/shard_map/reduce_scatter | solution.py:164
  131.7 1.0 copy-start.4
  171.9 3.0 copy-start.8
  172.1 2.8 copy-start.9
  197.9 7.7 %copy-start.2 = (bf16[8,64,4,128]{3,2,1,0:T(4,128)(2,1)}, bf16[8,64,4,128]{3,2,1,0:T(4,128)(2,1)S(1)}, u32[]{:S(2)}) copy-start(bf16[8,64,4,128]{3,2,1,0:T(4,128)(2,1)S(1)} %copy.53) | copy-start | bytes 1572868
  198.4 3.1 slice-start
  199.2 2.3 slice-start.1
  201.5 2.7 copy-start.7
  204.2 1.7 copy-start.6
  208.7 1.0 copy-start.3
  208.7 128.0 %reduce-scatter.5.cloned.1.call-start = ((), (), s32[]{:S(2)}) async-start(), calls=%async_computation.7 | async-start | bytes 10616832 | tf_op jit(solution)/shard_map/reduce_scatter | solution.py:141
  208.7 1.8 copy-start.12
  218.3 1.2 copy-start.5
  218.3 1.9 copy-start.13
  221.1 35.5 %copy-start = (bf16[128,2304]{1,0:T(8,128)(2,1)S(1)}, bf16[128,2304]{1,0:T(8,128)(2,1)}, u32[]{:S(2)}) copy-start(bf16[128,2304]{1,0:T(8,128)(2,1)} %param.6) | copy-start | bytes 1769476
  221.1 35.4 %copy-start.11 = (f32[2304]{0:T(1024)S(1)}, f32[2304]{0:T(1024)}, u32[]{:S(2)}) copy-start(f32[2304]{0:T(1024)} %param.8) | copy-start | bytes 27652
  336.7 2.3 copy-start.1
Sparse Core Ops, SparseCore 0:
  10.8 52.6 all-gather.4
  65.4 27.6 all-gather.6
  95.0 28.8 all-gather.10
  125.7 38.7 all-gather.8
  208.8 47.6 reduce-scatter.2
  259.9 76.7 reduce-scatter.4
where the time goes:
time: 348 us; the launch traced here: 347 us
  waiting for transfers between devices  208 us (60%)
  matrix products  51.2 us (15%)
  blocking collectives  40.3 us (12%)
  local copies, waits for them, and re-layouts  17.4 us (5%)
  other arithmetic  15.6 us (4%)
  between operations  14.5 us (4%)
    all_gather x1, waiting for transfers between devices, per_device(): gathered = lax.all_gather(normed_input, 'tensor', axis=0, tiled=True)  50.3 us
    psum x1, blocking collectives, per_device(): grad_pre = lax.psum(pre_part, ('dp', 'tensor'))  40.3 us
    reduce_scatter x1, waiting for transfers between devices, per_device(): lax.psum_scatter(lax.dot_general(block, joined, contract_first, preferred...  36.1 us
    reduce_scatter x1, waiting for transfers between devices, per_device(): lax.psum_scatter(total.astype(jnp.bfloat16), 'tensor', scatter_dimension=...  33.5 us
    all_gather x1, waiting for transfers between devices, per_device(): lax.all_gather(w_query, 'dp', axis=0, tiled=True)  29.7 us
    all_gather x1, waiting for transfers between devices, per_device(): lax.all_gather(value_weight, 'dp', axis=0, tiled=True)  29.6 us
    all_gather x1, waiting for transfers between devices, per_device(): lax.all_gather(key_weight, 'dp', axis=0, tiled=True)  26.8 us
    dot_general x3, matrix products, per_device(): jnp.dot(gathered, piece, preferred_element_type=jnp.float32)  13.8 us
  transfers between devices with their start and end apart: 6, of which 6 were waited for; matrix products, arithmetic and copies ran while one was open for 8% of the time, Pallas kernels for 0%

commit v1 on v0

--- a/solution.py
+++ b/solution.py
@@ -9,6 +9,17 @@
 CAP = 50.0
 BASE = 10000.0
 query_scalar = 144.0
+
+
+def turned_line(value, axis, dim):
+    size = lax.axis_size(axis)
+    forward = [(i, (i + 1) % size) for i in range(size)]
+    parts = [value]
+    for far in range(1, size):
+        parts = [lax.ppermute(parts[0], axis, forward), *parts]
+    whole = jnp.concatenate(parts, axis=dim)
+    turn = (lax.axis_index(axis) + 1) * parts[-1].shape[dim]
+    return jnp.roll(whole, turn, axis=dim)
 
 
 def rotary_tables(segment_length, half):
@@ -85,7 +96,7 @@
     inv_one = lax.rsqrt(jnp.mean(rows_f * rows_f, -1, keepdims=True) + EPS)
     unit_one = rows_f * inv_one
     normed_input = (unit_one * pre_gain).astype(jnp.bfloat16)
-    gathered = lax.all_gather(normed_input, "tensor", axis=0, tiled=True)
+    gathered = turned_line(normed_input, "tensor", 0)
     segment_length = gathered.shape[0]
     token_span = SEQ_LEN
     pieces_count = segment_length // token_span

time: 348 us -> 296 us (0.85)
  waiting for transfers between devices: 208 us -> 145 us
  matrix products: 51.2 us -> 55.4 us
  local copies, waits for them, and re-layouts: 17.4 us -> 21.4 us
    all_gather x1 -> x0, waiting for transfers between devices: 50.3 us -> none  [per_device(): gathered = lax.all_gather(normed_input, 'tensor', axis=0, tiled=True)]
    ppermute x0 -> x3, waiting for transfers between devices: none -> 45.4 us  [turned_line(): parts = [lax.ppermute(parts[0], axis, forward), *parts]]
    all_gather x1, waiting for transfers between devices: 29.6 us -> 0.01 us  [per_device(): lax.all_gather(value_weight, 'dp', axis=0, tiled=True)]
    all_gather x1, waiting for transfers between devices: 26.8 us -> 0.02 us  [per_device(): lax.all_gather(key_weight, 'dp', axis=0, tiled=True)]
    unnamed x36 -> x34, local copies, waits for them, and re-layouts: 6.72 us -> 11.8 us
  transfers between devices with their start and end apart: 6 -> 8, of which waited for: 6 -> 6; matrix products, arithmetic and copies ran while one was open for 8% -> 15% of each run, Pallas kernels for 0% -> 0%
where the time goes in v1:
time: 296 us; the launch traced here: 295 us
  waiting for transfers between devices  145 us (49%)
  matrix products  55.4 us (19%)
  blocking collectives  40.3 us (14%)
  local copies, waits for them, and re-layouts  21.4 us (7%)
  other arithmetic  15.5 us (5%)
  between operations  14.1 us (5%)
  starting transfers between devices  3.3 us (1%)
    ppermute x3, waiting for transfers between devices, turned_line(): parts = [lax.ppermute(parts[0], axis, forward), *parts]  45.4 us
    psum x1, blocking collectives, per_device(): grad_pre = lax.psum(pre_part, ('dp', 'tensor'))  40.3 us
    reduce_scatter x1, waiting for transfers between devices, per_device(): lax.psum_scatter(lax.dot_general(block, joined, contract_first, preferred...  36.1 us
    reduce_scatter x1, waiting for transfers between devices, per_device(): lax.psum_scatter(total.astype(jnp.bfloat16), 'tensor', scatter_dimension=...  32.4 us
    all_gather x1, waiting for transfers between devices, per_device(): lax.all_gather(w_query, 'dp', axis=0, tiled=True)  29.1 us
    dot_general x3, matrix products, per_device(): jnp.dot(gathered, piece, preferred_element_type=jnp.float32)  13.9 us
    unnamed x34, local copies, waits for them, and re-layouts  11.8 us
    dot_general x1, matrix products, per_device(): lax.dot_general(block, joined, contract_first, preferred_element_type=jnp...  9.4 us
  transfers between devices with their start and end apart: 8, of which 6 were waited for; matrix products, arithmetic and copies ran while one was open for 15% of the time, Pallas kernels for 0%

profile of v1, /device:TPU:0, one launch (start us, length us, event | category | flops | bytes accessed | tf_op | source)
XLA Modules:
  0.0 295.0 jit_solution(13423654210083702763)
XLA Ops:
  7.2 0.7 all-gather.4.cloned.1.call-update
  8.0 0.7 all-gather.8.cloned.1.call-update
  8.7 0.7 all-gather.6.cloned.1.call-update
  9.4 1.3 fusion.31
  10.7 0.9 fusion.29
  11.6 3.1 %collective-permute-start = (bf16[128,2304]{1,0:T(8,128)(2,1)S(1)}, bf16[128,2304]{1,0:T(8,128)(2,1)S(1)}, u32[]{:S(2)}, u32[]{:S(2)}) collective-permute-start(bf16[128,2304]{1,0:T(8,128)(2,1)S(1)} %fusion.29), channel_id=1, source_target_pairs={{0,1},{1,2},{2,3},{3,0},{4,5},{5,6},{6,7},{7,4},{8,9},{9,10},{10,1... | collective-permute-start | bytes 1769480 | tf_op jit(solution)/shard_map/ppermute | solution.py:19
  14.7 15.4 %collective-permute-done = bf16[128,2304]{1,0:T(8,128)(2,1)S(1)} collective-permute-done((bf16[128,2304]{1,0:T(8,128)(2,1)S(1)}, bf16[128,2304]{1,0:T(8,128)(2,1)S(1)}, u32[]{:S(2)}, u32[]{:S(2)}) %collective-permute-start) | collective-permute-done | bytes 589856 | tf_op jit(solution)/shard_map/ppermute | solution.py:19
  30.1 16.3 %collective-permute-done.1 = bf16[128,2304]{1,0:T(8,128)(2,1)S(1)} collective-permute-done((bf16[128,2304]{1,0:T(8,128)(2,1)S(1)}, bf16[128,2304]{1,0:T(8,128)(2,1)S(1)}, u32[]{:S(2)}, u32[]{:S(2)}) %collective-permute-start.1) | collective-permute-done | bytes 589856 | tf_op jit(solution)/shard_map/ppermute | solution.py:19
  46.4 1.5 copy.62
  48.1 13.7 %collective-permute-done.2 = bf16[128,2304]{1,0:T(8,128)(2,1)S(1)} collective-permute-done((bf16[128,2304]{1,0:T(8,128)(2,1)S(1)}, bf16[128,2304]{1,0:T(8,128)(2,1)S(1)}, u32[]{:S(2)}, u32[]{:S(2)}) %collective-permute-start.2) | collective-permute-done | bytes 589856 | tf_op jit(solution)/shard_map/ppermute | solution.py:19
  61.8 0.8 constant_dynamic-update-slice_fusion.7
  62.7 0.9 constant_dynamic-update-slice_fusion.6
  63.5 0.9 constant_dynamic-update-slice_fusion.5
  64.4 1.0 constant_dynamic-update-slice_fusion.4
  65.4 0.9 constant_dynamic-update-slice_fusion.3
  66.3 0.8 constant_dynamic-update-slice_fusion.2
  67.2 0.9 constant_dynamic-update-slice_fusion.1
  68.0 1.0 constant_dynamic-update-slice_fusion
  69.0 3.8 %fusion.24 = bf16[512,512]{1,0:T(8,128)(2,1)S(1)} fusion(bf16[2304,512]{1,0:T(8,128)(2,1)} %all-gather.4.cloned.1.call-done, bf16[1024,2304]{1,0:T(8,128)(2,1)} %constant_dynamic-update-slice_fusion, s32[]{:T(128)S(6)} %select_n.18), kind=kOutput, calls=%fused_computation.42 | convolution fusion | flops 1208221696 | bytes 5242884 | tf_op jit(solution)/shard_map/dot_general | solution.py:111
  73.1 4.7 %fusion.12 = f32[512,512]{1,0:T(8,128)} fusion(bf16[2304,512]{1,0:T(8,128)(2,1)} %all-gather.8.cloned.1.call-done, bf16[1024,2304]{1,0:T(8,128)(2,1)} %constant_dynamic-update-slice_fusion, s32[]{:T(128)S(6)} %select_n.18), kind=kOutput, calls=%fused_computation.25 | convolution fusion | flops 1207959552 | bytes 5767172 | tf_op jit(solution)/shard_map/dot_general | solution.py:111
  77.9 1.6 reshape.112
  79.4 0.6 fusion.68
  80.1 0.3 subtract_convert_fusion.3
  80.4 0.3 pad_maximum_fusion.2
  80.7 0.2 broadcast_in_dim.12
  81.0 1.0 copy-done.3
  81.9 2.0 fusion.37
  83.9 29.1 %all-gather.6.cloned.1.call-done = bf16[2304,1024]{1,0:T(8,128)(2,1)} async-done(((bf16[288,1024]{1,0:T(8,128)(2,1)}), bf16[2304,1024]{1,0:T(8,128)(2,1)}) %all-gather.6.cloned.1.call-update) | async-done | bytes 4718608 | tf_op jit(solution)/shard_map/all_gather | solution.py:106
  113.0 5.3 %convolution_bitcast_fusion = f32[64,8,8,128]{3,1,2,0:T(8,128)S(1)} fusion(bf16[2304,1024]{1,0:T(8,128)(2,1)} %all-gather.6.cloned.1.call-done, bf16[1024,2304]{1,0:T(8,128)(2,1)} %constant_dynamic-update-slice_fusion, s32[]{:T(128)S(6)} %select_n.18), kind=kOutput, calls=%fused_computation.22 | convolution fusion | flops 2415919104 | bytes 9175044 | tf_op jit(solution)/shard_map/dot_general | solution.py:111
  118.4 0.5 copy.60
  118.8 0.7 fusion.66
  119.5 0.9 subtract_convert_fusion.1
  120.4 0.2 broadcast_in_dim.18
  120.7 2.6 fusion.18
  123.3 7.3 %fusion.34 = f32[8,8,128,64]{2,3,1,0:T(8,128)} fusion(f32[8,8,64,64]{3,2,1,0:T(8,128)} %fusion.37, f32[8,8,64,64]{2,3,1,0:T(8,128)} %get-tuple-element.25, bf16[8,64,8,64]{3,1,2,0:T(8,128)(2,1)} %copy-done.7, bf16[8,64,8,64]{3,1,2,0:T(8,128)(2,1)S(1)} %get-tuple-element.8, f32[8,8,64]{2,1,0:T(8,128)S(1)} %get-tuple-element.24, ...), kind=kOutput, calls=%fused_computation.58 | convolution fusion | flops 73404480 | bytes 5263360 | tf_op jit(solution)/shard_map/vmap(hqk,qhd->khd)/dot_general | solution.py:76
  130.6 7.0 %convolution_bitcast_fusion.1 = f32[8,64,8,128]{3,1,2,0:T(8,128)} fusion(bf16[8,64,8,128]{3,1,2,0:T(8,128)(2,1)} %bitcast.87, f32[8,8,64,64]{3,2,1,0:T(8,128)} %fusion.37, f32[8,8,64,64]{2,3,1,0:T(8,128)} %get-tuple-element.25, f32[8,8,64]{2,1,0:T(8,128)S(1)} %get-tuple-element.24, pred[64,64]{0,1:T(8,128)(4,1)S(1)} %iota_compare_fusion), kind=kOutput, calls=%fused_computation.23 | convolution fusion | flops 71307328 | bytes 5263360 | tf_op jit(solution)/shard_map/vmap(hqk,khd->qhd)/dot_general | solution.py:75
  137.7 3.7 %fusion.35 = f32[8,8,64,128]{3,2,1,0:T(8,128)} fusion(bf16[8,64,8,128]{3,2,1,0:T(8,128)(2,1)S(1)} %bitcast.83, f32[8,8,64,64]{2,3,1,0:T(8,128)} %get-tuple-element.25, f32[8,8,64]{2,1,0:T(8,128)S(1)} %get-tuple-element.24, pred[64,64]{0,1:T(8,128)(4,1)S(1)} %iota_compare_fusion), kind=kOutput, calls=%fused_computation.59 | convolution fusion | flops 68419584 | bytes 4214784 | tf_op jit(solution)/shard_map/vmap(hqk,qhd->khd)/dot_general | solution.py:77
  141.3 1.9 reduce_sum.66
  143.2 1.8 reduce_sum.67
  145.0 0.4 copy.53
  145.4 0.4 add_convert_fusion.2
  145.9 0.7 copy-done.1
  146.6 0.8 add_convert_fusion
  147.4 0.6 pad_maximum_fusion.1
  148.0 0.9 copy.50
  148.9 0.3 pad_maximum_fusion.3
  149.2 0.4 copy.51
  149.7 2.7 fusion.59
  152.4 1.4 convolution_add_fusion.1
  153.8 0.2 copy-done.5
  154.0 2.9 fusion.1
  157.0 0.3 copy.85
  157.4 9.4 %convolution_convert_fusion = bf16[2304,2048]{1,0:T(8,128)(2,1)} fusion(bf16[512,512]{1,0:T(8,128)(2,1)S(1)} %get-tuple-element.26, bf16[512,512]{1,0:T(8,128)(2,1)S(1)} %get-tuple-element.27, bf16[512,1024]{1,0:T(8,128)(2,1)S(1)} %bitcast.90, bf16[1024,2304]{1,0:T(8,128)(2,1)} %constant_dynamic-update-slice_fusion, s32[]{:T(128)S(6)} %select_n.18), kind=kOutput, calls=%fused_computation.1 | convolution fusion | flops 4842848256 | bytes 13893636 | tf_op jit(solution)/shard_map/dot_general | solution.py:153
  166.9 1.2 copy-done.4
  168.1 2.4 fusion.23
  170.5 0.7 copy.47
  171.2 1.2 copy.86
  172.5 32.4 %reduce-scatter.3.cloned.1.call-done = bf16[128,2304]{1,0:T(8,128)(2,1)} async-done(((bf16[512,2304]{1,0:T(8,128)(2,1)}), bf16[128,2304]{1,0:T(8,128)(2,1)}) %reduce-scatter.3.cloned.1.call-update) | async-done | bytes 589840 | tf_op jit(solution)/shard_map/reduce_scatter | solution.py:175
  204.8 1.5 fusion.32
  206.3 40.3 %psum.7 = f32[2304]{0:T(1024)} all-reduce(f32[2304]{0:T(1024)S(1)} %get-tuple-element.6), channel_id=1, replica_groups=mesh['dp'=8,'tensor'=4] {'dp','tensor'}, use_global_device_ids=true, to_apply=%region_9.10 | all-reduce | flops 2304 | bytes 18432 | tf_op jit(solution)/shard_map/psum | solution.py:183
  246.6 2.3 fusion.28
  248.9 36.1 %reduce-scatter.5.cloned.1.call-done = bf16[288,2048]{1,0:T(8,128)(2,1)} async-done(((bf16[2304,2048]{1,0:T(8,128)(2,1)}), bf16[288,2048]{1,0:T(8,128)(2,1)}) %reduce-scatter.5.cloned.1.call-update) | async-done | bytes 1179664 | tf_op jit(solution)/shard_map/reduce_scatter | solution.py:152
  285.0 2.3 slice.52
  287.3 1.2 fusion.67
  (40 shorter events, 0.9 us)
Async XLA Ops:
  7.2 3.6 %copy-start = (bf16[128,2304]{1,0:T(8,128)(2,1)S(1)}, bf16[128,2304]{1,0:T(8,128)(2,1)}, u32[]{:S(2)}) copy-start(bf16[128,2304]{1,0:T(8,128)(2,1)} %param.6) | copy-start | bytes 1769476
  7.2 61.9 %all-gather.4.cloned.1.call-start = ((), (), s32[]{:S(2)}) async-start(), calls=%async_computation.2 | async-start | bytes 2654208 | tf_op jit(solution)/shard_map/all_gather | solution.py:108
  7.9 65.2 %all-gather.8.cloned.1.call-start = ((), (), s32[]{:S(2)}) async-start(), calls=%async_computation.4 | async-start | bytes 2654208 | tf_op jit(solution)/shard_map/all_gather | solution.py:107
  8.7 104.4 %all-gather.6.cloned.1.call-start = ((), (), s32[]{:S(2)}) async-start(), calls=%async_computation.3 | async-start | bytes 5308416 | tf_op jit(solution)/shard_map/all_gather | solution.py:106
  9.4 195.4 %reduce-scatter.3.cloned.1.call-start = ((), (), s32[]{:S(2)}) async-start(), calls=%async_computation.5 | async-start | bytes 2949120 | tf_op jit(solution)/shard_map/reduce_scatter | solution.py:175
  11.6 18.5 %collective-permute-start = (bf16[128,2304]{1,0:T(8,128)(2,1)S(1)}, bf16[128,2304]{1,0:T(8,128)(2,1)S(1)}, u32[]{:S(2)}, u32[]{:S(2)}) collective-permute-start(bf16[128,2304]{1,0:T(8,128)(2,1)S(1)} %fusion.29), channel_id=1, source_target_pairs={{0,1},{1,2},{2,3},{3,0},{4,5},{5,6},{6,7},{7,4},{8,9},{9,10},{10,1... | collective-permute-start | bytes 1769480 | tf_op jit(solution)/shard_map/ppermute | solution.py:19
  30.1 16.3 %collective-permute-start.1 = (bf16[128,2304]{1,0:T(8,128)(2,1)S(1)}, bf16[128,2304]{1,0:T(8,128)(2,1)S(1)}, u32[]{:S(2)}, u32[]{:S(2)}) collective-permute-start(bf16[128,2304]{1,0:T(8,128)(2,1)S(1)} %collective-permute-done), channel_id=1, source_target_pairs={{0,1},{1,2},{2,3},{3,0},{4,5},{5,6},{6,7},{7,4},{8,9},{9,10},{10,1... | collective-permute-start | bytes 1769480 | tf_op jit(solution)/shard_map/ppermute | solution.py:19
  46.4 15.4 %collective-permute-start.2 = (bf16[128,2304]{1,0:T(8,128)(2,1)S(1)}, bf16[128,2304]{1,0:T(8,128)(2,1)S(1)}, u32[]{:S(2)}, u32[]{:S(2)}) collective-permute-start(bf16[128,2304]{1,0:T(8,128)(2,1)S(1)} %collective-permute-done.1), channel_id=1, source_target_pairs={{0,1},{1,2},{2,3},{3,0},{4,5},{5,6},{6,7},{7,4},{8,9},{9,10},{10,1... | collective-permute-start | bytes 1769480 | tf_op jit(solution)/shard_map/ppermute | solution.py:19
  47.9 16.5 %copy-start.9 = (f32[2304]{0:T(1024)S(1)}, f32[2304]{0:T(1024)}, u32[]{:S(2)}) copy-start(f32[2304]{0:T(1024)} %param.8) | copy-start | bytes 27652
  81.0 1.0 copy-start.3
  120.4 2.9 copy-start.7
  120.7 2.7 copy-start.8
  145.0 1.6 copy-start.1
  146.6 3.1 %slice-start = ((s8[4718592]{0:T(1024)(128)(4,1)}), s8[4194304]{0:T(1024)(128)(4,1)S(1)}, s32[]{:S(2)}) async-start(s8[4718592]{0:T(1024)(128)(4,1)} %bitcast.91), calls=%async_computation.7 | async-start | bytes 8388608
  147.4 2.3 slice-start.1
  149.7 2.7 copy-start.6
  152.4 1.7 copy-start.5
  157.0 128.1 %reduce-scatter.5.cloned.1.call-start = ((), (), s32[]{:S(2)}) async-start(), calls=%async_computation.6 | async-start | bytes 10616832 | tf_op jit(solution)/shard_map/reduce_scatter | solution.py:152
  166.8 1.2 copy-start.4
  285.0 2.3 copy-start.2
Sparse Core Ops, SparseCore 0:
  9.9 31.5 all-gather.3
  43.4 28.8 all-gather.7
  74.2 38.7 all-gather.5
  157.1 47.6 reduce-scatter.2
  208.2 76.8 reduce-scatter.4
